TPU v7x, 32 devices: a whole 2x2x4 slice. The times are simulated.
32 devices in a mesh: ep: 8 (over z, x), fsdp: 4 (over y, core).
Axes of the slice: x: 2, y: 2, z: 4, core: 2. Of those that a mesh axis runs over, the one named last changes fastest.
Arguments:
- train_down: float32 [64, 1408, 2048], P('ep', None, 'fsdp'), may hold values from -0.21875 to 0.21875
- other_down: float32 [64, 1408, 2048], P('ep', None, 'fsdp'), may hold values from -0.15625 to 0.15625
- router_weight: float32 [2048, 64], P('fsdp', 'ep'), may hold values from -0.125 to 0.125
- router_gain: float32 [2048], P('fsdp'), may hold values from 0.25 to 1.75
Outputs:
- ready_down: bfloat16 [64, 1408, 2048], P('ep')
- scale_down: float32 [64, 1408], P('ep')
- serve_router: bfloat16 [2048, 64], replicated
- latest_down: float32 [64, 1408, 2048], P('ep', None, 'fsdp')
All inputs are finite; a program needn't handle non-finite values.
Results may differ from a plain program's by a relative error of at most 0.001.
Values may be sent and summed in bfloat16 or wider, within the bound.
No kernel may reach another device: no remote copies, remote signals or barrier semaphores. Data moves between devices by JAX's collectives and lax.ppermute only.
A program may use at most 256 MiB of HBM per device.

v0:
```python
import jax
import jax.numpy as jnp
from jax import lax
from jax.sharding import PartitionSpec as P


def on_device(train_down, other_down, router_weight, router_gain):
    latest_down = 0.5 * other_down + 0.5 * train_down
    total_down = lax.psum(jnp.sum(latest_down * latest_down, axis=2), "fsdp")
    scale_down = jnp.sqrt(total_down)
    narrow_down = (latest_down / jnp.expand_dims(scale_down, 2)).astype(jnp.bfloat16)
    ready_down = lax.all_gather(narrow_down, "fsdp", axis=2, tiled=True)
    part_router = (router_weight * router_gain[:, None]).astype(jnp.bfloat16)
    row_router = lax.all_gather(part_router, "fsdp", axis=0, tiled=True)
    serve_router = lax.all_gather(row_router, "ep", axis=1, tiled=True)
    return (ready_down, scale_down, serve_router, latest_down)


def solution(mesh):
    placed = (P("ep", None, "fsdp"), P("ep", None, "fsdp"), P("fsdp", "ep"), P("fsdp"))
    return jax.shard_map(
        on_device,
        mesh=mesh,
        in_specs=placed,
        out_specs=(P("ep", None, None), P("ep", None), P(), P("ep", None, "fsdp")),
        check_vma=False,
    )
```

profile of v0, /device:TPU:0, one launch (start us, length us, event | category | flops | bytes accessed | tf_op | source)
XLA Modules:
  0.0 368.7 jit_solution(947301577113018860)
XLA Ops:
  7.2 0.0 all-gather.2.cloned.1.call-start
  7.2 22.7 %multiply_reduce_fusion = (f32[8,1408]{1,0:T(8,128)S(1)}, f32[8,1408,512]{2,1,0:T(8,128)}) fusion(f32[8,1408,512]{2,1,0:T(8,128)} %param.5, f32[8,1408,512]{2,1,0:T(8,128)} %param.4), kind=kLoop, calls=%fused_computation.1 | loop fusion | flops 23057408 | bytes 69251072 | tf_op jit(solution)/shard_map/reduce_sum | solution.py:9
  29.9 13.2 %psum.7 = f32[8,1408]{1,0:T(8,128)S(1)} all-reduce(f32[8,1408]{1,0:T(8,128)S(1)} %get-tuple-element.4), channel_id=1, replica_groups=mesh['ep'=8,'fsdp'=4] {'fsdp'}, use_global_device_ids=true, to_apply=%region_1.0 | all-reduce | flops 11264 | bytes 90112 | tf_op jit(solution)/shard_map/psum | solution.py:9
  43.2 0.0 copy-start
  43.2 0.0 copy-start.1
  43.2 0.0 copy-start.2
  43.2 13.0 %divide_convert_fusion = bf16[8,1408,512]{2,1,0:T(8,128)(2,1)} fusion(f32[8,1408,512]{2,1,0:T(8,128)} %get-tuple-element.13, f32[8,1408]{1,0:T(8,128)S(1)} %sqrt.3), kind=kLoop, calls=%fused_computation | loop fusion | flops 11534336 | bytes 34648064 | tf_op jit(solution)/shard_map/convert_element_type | solution.py:11
  56.2 0.0 all-gather.2.cloned.1.call-update
  56.3 0.0 copy-done
  56.3 0.0 copy-done.1
  56.3 0.0 copy-done.2
  56.3 5.2 %all_gather.10 = bf16[2048,8]{0,1:T(8,128)(2,1)S(1)} all-gather(bf16[512,8]{0,1:T(8,128)(2,1)S(1)} %multiply_convert_fusion), channel_id=1, replica_groups=mesh['ep'=8,'fsdp'=4] {'fsdp'}, dimensions={0}, use_global_device_ids=true | all-gather | bytes 40960 | tf_op jit(solution)/shard_map/all_gather | solution.py:14
  61.5 31.2 %all_gather.11 = bf16[2048,64]{0,1:T(8,128)(2,1)S(1)} all-gather(bf16[2048,8]{0,1:T(8,128)(2,1)S(1)} %all_gather.10), channel_id=1, replica_groups=mesh['ep'=8,'fsdp'=4] {'ep'}, dimensions={1}, use_global_device_ids=true | all-gather | bytes 294912 | tf_op jit(solution)/shard_map/all_gather | solution.py:15
  92.7 237.6 %all-gather.2.cloned.1.call-done = bf16[8,1408,2048]{2,1,0:T(8,128)(2,1)} async-done(((bf16[8,1408,512]{2,1,0:T(8,128)(2,1)}), bf16[8,1408,2048]{2,1,0:T(8,128)(2,1)}) %all-gather.2.cloned.1.call-update) | async-done | bytes 46137360 | tf_op jit(solution)/shard_map/all_gather | solution.py:12
  330.3 30.8 %copy.10 = bf16[8,1408,2048]{2,1,0:T(8,128)(2,1)} copy(bf16[8,1408,2048]{2,1,0:T(8,128)(2,1)} %all-gather.2.cloned.1.call-done) | data formatting | bytes 92274688
  361.1 0.7 copy.11
  (2 shorter events, 0.0 us)
Async XLA Ops:
  7.2 323.1 %all-gather.2.cloned.1.call-start = ((), (), s32[]{:S(2)}) async-start(), calls=%async_computation | async-start | bytes 57671680 | tf_op jit(solution)/shard_map/all_gather | solution.py:12
  43.2 13.1 %copy-start = (f32[8,1408]{1,0:T(8,128)}, f32[8,1408]{1,0:T(8,128)S(1)}, u32[]{:S(2)}) copy-start(f32[8,1408]{1,0:T(8,128)S(1)} %sqrt.3) | copy-start | bytes 135172
  43.2 13.1 %copy-start.1 = (f32[512,8]{0,1:T(8,128)S(1)}, f32[512,8]{0,1:T(8,128)}, u32[]{:S(2)}) copy-start(f32[512,8]{0,1:T(8,128)} %param.6) | copy-start | bytes 49156
  43.2 13.1 %copy-start.2 = (f32[512]{0:T(512)S(1)}, f32[512]{0:T(512)}, u32[]{:S(2)}) copy-start(f32[512]{0:T(512)} %param.7) | copy-start | bytes 6148
Sparse Core Ops, SparseCore 0:
  56.4 273.8 all-gather.1
where the time goes:
time: 369 us
  waiting for transfers between devices  238 us (64%)
  blocking collectives  49.6 us (13%)
  other arithmetic  35.7 us (10%)
  local copies, waits for them, and re-layouts  31.6 us (9%)
  between operations  14.1 us (4%)
    all_gather x1, waiting for transfers between devices, on_device(): ready_down = lax.all_gather(narrow_down, 'fsdp', axis=2, tiled=True)  238 us
    unnamed x8, local copies, waits for them, and re-layouts  31.6 us
    all_gather x1, blocking collectives, on_device(): serve_router = lax.all_gather(row_router, 'ep', axis=1, tiled=True)  31.2 us
    reduce_sum x1, other arithmetic, on_device(): total_down = lax.psum(jnp.sum(latest_down * latest_down, axis=2), 'fsdp')  22.7 us
    psum x1, blocking collectives, on_device(): total_down = lax.psum(jnp.sum(latest_down * latest_down, axis=2), 'fsdp')  13.2 us
    convert_element_type x1, other arithmetic, on_device(): (latest_down / jnp.expand_dims(scale_down, 2)).astype(jnp.bfloat16)  13 us
  transfers between devices with their start and end apart: 1, of which 1 were waited for; matrix products, arithmetic and copies ran while one was open for 0% of the time, Pallas kernels for 0%

commit v1 on v0

v1 whole, which is shorter than its diff:
```python
import functools

import jax
import jax.numpy as jnp
from jax import lax
from jax.experimental import pallas as pl
from jax.experimental.pallas import tpu as pltpu
from jax.sharding import PartitionSpec as P


PARTS = 16
PIECES = (1, 1, 2, 2, 2, 2, 2, 2, 1, 1)
FIRST = 3


def place_kernel(count, columns_ref, *refs):
    ready_ref = refs[-1]
    for index in range(count):
        width = refs[index].shape[1]
        start = pl.multiple_of(columns_ref[index] * width, width)
        ready_ref[:, pl.ds(start, width)] = refs[index][...]


def place(columns, blocks, ready, start, rows, step):
    count = len(blocks)
    size, width = blocks[0].shape
    at = start // step
    in_specs = [pl.BlockSpec((step, width), lambda i, c: (i, 0)) for _ in blocks]
    args = [columns, *blocks]
    aliases = {}
    if ready is not None:
        in_specs.append(pl.BlockSpec(memory_space=pl.ANY))
        args.append(ready)
        aliases = {count + 1: 0}
    return pl.pallas_call(
        functools.partial(place_kernel, count),
        grid_spec=pltpu.PrefetchScalarGridSpec(
            num_scalar_prefetch=1,
            grid=(size // step,),
            in_specs=in_specs,
            out_specs=pl.BlockSpec((step, count * width), lambda i, c: (at + i, 0)),
        ),
        out_shape=jax.ShapeDtypeStruct((rows, count * width), blocks[0].dtype),
        input_output_aliases=aliases,
        cost_estimate=pl.CostEstimate(
            flops=4 * size * count * width,
            bytes_accessed=4 * size * count * width,
            transcendentals=0,
        ),
    )(*args)


def on_device(n, train_down, other_down, router_weight, router_gain):
    experts, inner, width = train_down.shape
    rows = experts * inner
    chips = n // 2
    me = lax.axis_index("fsdp")

    def send(values, hop, swap):
        pairs = [(i, ((i // 2 + hop) % chips) * 2 + ((i % 2) ^ swap)) for i in range(n)]
        return lax.ppermute(values, "fsdp", pairs)

    hops = [(hop, swap) for hop in range(chips) for swap in range(2)]
    behind = jnp.array([chips - hop for hop, _ in hops], jnp.int32) + (me >> 1)
    behind = jnp.where(behind >= chips, behind - chips, behind)
    columns = behind * 2 + ((me & 1) ^ jnp.array([swap for _, swap in hops], jnp.int32))

    def total(part):
        if n != 4:
            return lax.psum(part, "fsdp")
        near = part + send(part, 0, 1)
        far = send(part, 1, 0) + send(part, 1, 1)
        return near + far

    train = train_down.reshape(rows, width)
    other = other_down.reshape(rows, width)

    def latest(first, last, train, other):
        return 0.5 * other[first:last] + 0.5 * train[first:last]

    def squares(first, last, train, other):
        part = latest(first, last, train, other)
        return jnp.sum(part * part, axis=1)

    unit = rows // PARTS
    step = unit // 2 if unit % 32 == 0 else unit
    edges = [0]
    for piece in PIECES:
        edges.append(edges[-1] + piece * unit)
    split = edges[FIRST]

    def narrow(index, scale, base, train, other):
        first, last = edges[index], edges[index + 1]
        return (latest(first, last, train, other) / scale[first - base:last - base, None]).astype(jnp.bfloat16)

    part_router = (router_weight * router_gain[:, None]).astype(jnp.bfloat16).T
    router_blocks = [part_router if hop == (0, 0) else send(part_router, *hop) for hop in hops]

    scale_first = jnp.sqrt(total(squares(0, split, train, other)))
    own = [narrow(i, scale_first, 0, train, other) for i in range(FIRST)]
    own[0], own[1], train, other, *router_blocks = lax.optimization_barrier(
        (own[0], own[1], train, other, *router_blocks)
    )
    part_rest = squares(split, rows, train, other)
    part_rest, own[2] = lax.optimization_barrier((part_rest, own[2]))
    scale_rest = jnp.sqrt(total(part_rest))
    own += [narrow(i, scale_rest, split, train, other) for i in range(FIRST, len(PIECES))]

    high, _ = part_router.shape
    row_router = place(columns, router_blocks, None, 0, high, high)
    row_router, own[3] = lax.optimization_barrier((row_router, own[3]))
    all_router = lax.all_gather(row_router, "ep", axis=0, tiled=True)

    far, ready = {}, None
    for index in range(len(own) + 1):
        if index < len(own):
            if index >= 2:
                own[index], *far[index - 2] = lax.optimization_barrier((own[index], *far[index - 2]))
            if index >= 3:
                own[index], ready = lax.optimization_barrier((own[index], ready))
            if index == 5:
                own[index], all_router = lax.optimization_barrier((own[index], all_router))
                train, other, ready = lax.optimization_barrier((train, other, ready))
                latest_down = latest(0, rows, train, other)
            if index == 7:
                own[index], latest_down = lax.optimization_barrier((own[index], latest_down))
            far[index] = [send(own[index], hop, 0) for hop in range(1, chips)]
        done = index - 2
        for at in [done] if index < len(own) else [done, done + 1]:
            if at < 0:
                continue
            blocks = []
            for arrived in [own[at], *far[at]]:
                blocks += [arrived, send(arrived, 0, 1)]
            ready = place(columns, blocks, ready, edges[at], rows, step)

    latest_down = latest_down.reshape(experts, inner, width)
    serve_router = all_router.T

    scale_down = jnp.concatenate([scale_first, scale_rest]).reshape(experts, inner)
    return (ready.reshape(experts, inner, n * width), scale_down, serve_router, latest_down)


def solution(mesh):
    placed = (P("ep", None, "fsdp"), P("ep", None, "fsdp"), P("fsdp", "ep"), P("fsdp"))

    def body(*args):
        return on_device(mesh.shape["fsdp"], *args)

    return jax.shard_map(
        body,
        mesh=mesh,
        in_specs=placed,
        out_specs=(P("ep", None, None), P("ep", None), P(), P("ep", None, "fsdp")),
        check_vma=False,
    )
```

time: 369 us -> 324 us (0.88)
  waiting for transfers between devices: 238 us -> 147 us
  Pallas kernels: 0 us -> 54.3 us
  other arithmetic: 35.7 us -> 65.5 us
  local copies, waits for them, and re-layouts: 31.6 us -> 2.44 us
  starting transfers between devices: 0.04 us -> 19.7 us
  blocking collectives: 49.6 us -> 33.1 us
  between operations: 14.1 us -> 0.91 us
    all_gather x1 -> x0, waiting for transfers between devices: 238 us -> none  [on_device(): ready_down = lax.all_gather(narrow_down, 'fsdp', axis=2, tiled=True)]
    ppermute x0 -> x39, waiting for transfers between devices: none -> 147 us  [send(): return lax.ppermute(values, 'fsdp', pairs)]
    pallas_call x0 -> x11, Pallas kernels: none -> 54.3 us  [place(): pl.pallas_call(functools.partial(place_kernel, count), grid_spec=pltpu.Pr...]
    unnamed x8 -> x39, local copies, waits for them, and re-layouts: 31.6 us -> 1.64 us
    add x0 -> x2, other arithmetic: none -> 23.4 us  [the longest x1 22.8 us: latest(): return 0.5 * other[first:last] + 0.5 * train[first:last]]
    ppermute x0 -> x39, starting transfers between devices: none -> 19.7 us  [send(): return lax.ppermute(values, 'fsdp', pairs)]
    psum x1 -> x0, blocking collectives: 13.2 us -> none  [on_device(): total_down = lax.psum(jnp.sum(latest_down * latest_down, axis=2), 'fsdp')]
    convert_element_type x2 -> x4, other arithmetic: 13.1 us -> 25.1 us  [narrow(): (latest(first, last, train, other) / scale[first - base:last - base, None...]
  transfers between devices with their start and end apart: 1 -> 39, of which waited for: 1 -> 10; matrix products, arithmetic and copies ran while one was open for 0% -> 14% of each run, Pallas kernels for 0% -> 16%
where the time goes in v1:
time: 324 us; the launch traced here: 323 us
  waiting for transfers between devices  147 us (45%)
  other arithmetic  65.5 us (20%)
  Pallas kernels  54.3 us (17%)
  blocking collectives  33.1 us (10%)
  starting transfers between devices  19.7 us (6%)
    ppermute x39, waiting for transfers between devices, send(): return lax.ppermute(values, 'fsdp', pairs)  147 us
    pallas_call x11, Pallas kernels, place(): pl.pallas_call(functools.partial(place_kernel, count), grid_spec=pltpu.Pr...  54.3 us
    all_gather x1, blocking collectives, on_device(): all_router = lax.all_gather(row_router, 'ep', axis=0, tiled=True)  33.1 us
    convert_element_type x4, other arithmetic, narrow(): (latest(first, last, train, other) / scale[first - base:last - base, None...  25.1 us
    add x1, other arithmetic, latest(): return 0.5 * other[first:last] + 0.5 * train[first:last]  22.8 us
    ppermute x39, starting transfers between devices, send(): return lax.ppermute(values, 'fsdp', pairs)  19.7 us
    reduce_sum x2, other arithmetic, squares(): return jnp.sum(part * part, axis=1)  17 us
  transfers between devices with their start and end apart: 39, of which 10 were waited for; matrix products, arithmetic and copies ran while one was open for 14% of the time, Pallas kernels for 16%

profile of v1, /device:TPU:0, one launch (start us, length us, event | category | flops | bytes accessed | tf_op | source)
XLA Modules:
  0.0 323.1 jit_solution(2495227278794638044)
XLA Ops:
  0.7 5.2 %multiply_reduce_fusion.1 = f32[2,1408]{1,0:T(2,128)S(1)} fusion(f32[8,1408,512]{2,1,0:T(8,128)} %param.6, f32[8,1408,512]{2,1,0:T(8,128)} %param.7), kind=kLoop, calls=%fused_computation.2 | loop fusion | flops 5764352 | bytes 11545600 | tf_op jit(solution)/shard_map/reduce_sum | solution.py:83
  12.2 4.3 %fusion.6 = (bf16[704,512]{1,0:T(8,128)(2,1)}, bf16[704,512]{1,0:T(8,128)(2,1)}) fusion(f32[11264,512]{1,0:T(8,128)} %bitcast.12, f32[11264,512]{1,0:T(8,128)} %bitcast.17, f32[704]{0:T(1024)S(1)} %get-tuple-element.118, f32[704]{0:T(1024)S(1)} %get-tuple-element.119), kind=kLoop, calls=%fused_computation.19 | loop fusion | flops 2883584 | bytes 7214592 | tf_op jit(solution)/shard_map/convert_element_type | solution.py:94
  16.5 4.2 %fusion.refs_0_ = bf16[1408,512]{1,0:T(8,128)(2,1)} fusion(f32[8,1408,512]{2,1,0:T(8,128)} %param.6, f32[8,1408,512]{2,1,0:T(8,128)} %param.7, f32[1408]{0:T(1024)S(1)} %slice.146), kind=kLoop, calls=%fused_computation.4 | loop fusion | flops 2883584 | bytes 7214592 | tf_op jit(solution)/shard_map/convert_element_type | solution.py:94
  20.8 11.8 %multiply_reduce_fusion = f32[8448]{0:T(1024)S(1)} fusion(f32[11264,512]{1,0:T(8,128)} %bitcast.13, f32[11264,512]{1,0:T(8,128)} %bitcast.18), kind=kLoop, calls=%fused_computation.1 | loop fusion | flops 17293056 | bytes 34636800 | tf_op jit(solution)/shard_map/reduce_sum | solution.py:83
  39.4 14.5 %collective-permute-done.11.refs_2_ = bf16[704,512]{1,0:T(8,128)(2,1)} collective-permute-done((bf16[704,512]{1,0:T(8,128)(2,1)}, bf16[704,512]{1,0:T(8,128)(2,1)}, u32[]{:S(2)}, u32[]{:S(2)}) %collective-permute-start.11) | collective-permute-done | bytes 720928 | tf_op jit(solution)/shard_map/ppermute | solution.py:61
  54.7 12.4 %divide_convert_fusion = (bf16[1408,512]{1,0:T(8,128)(2,1)S(1)}, bf16[1408,512]{1,0:T(8,128)(2,1)}, bf16[1408,512]{1,0:T(8,128)(2,1)}, bf16[1408,512]{1,0:T(8,128)(2,1)}, bf16[1408,512]{1,0:T(8,128)(2,1)S(1)}) fusion(f32[11264,512]{1,0:T(8,128)} %bitcast.14, f32[11264,512]{1,0:T(8,128)} %bitcast.19, f32[1408]{0:T(1024)S(1)} %get-tuple-element.113, ...), kind=kLoop, calls=%fused_computation.5 | loop fusion | flops 14417920 | bytes 36072960 | tf_op jit(solution)/shard_map/convert_element_type | solution.py:94
  74.4 25.9 %collective-permute-done.15.refs_2_ = bf16[1408,512]{1,0:T(8,128)(2,1)} collective-permute-done((bf16[1408,512]{1,0:T(8,128)(2,1)}, bf16[1408,512]{1,0:T(8,128)(2,1)}, u32[]{:S(2)}, u32[]{:S(2)}) %collective-permute-start.15) | collective-permute-done | bytes 1441824 | tf_op jit(solution)/shard_map/ppermute | solution.py:61
  100.3 3.7 %shard_map.95.refs_4_ = bf16[11264,2048]{1,0:T(8,128)(2,1)} custom-call(s32[4]{0:T(128)} %fusion.9.columns_ref, bf16[704,512]{1,0:T(8,128)(2,1)} %get-tuple-element.61.refs_0_, bf16[704,512]{1,0:T(8,128)(2,1)} %collective-permute-done.17.refs_1_, bf16[704,512]{1,0:T(8,128)(2,1)} %collective-permute-done.9.refs_2_, ...), custom_call_target="tpu_custom_call", output_to_operand_aliasing={{}: (5, {})} | custom-call | flops 5767168 | bytes 5767168 | tf_op jit(solution)/shard_map/pallas_call | solution.py:35
  105.0 26.1 %collective-permute-done.13.refs_2_ = bf16[1408,512]{1,0:T(8,128)(2,1)} collective-permute-done((bf16[1408,512]{1,0:T(8,128)(2,1)}, bf16[1408,512]{1,0:T(8,128)(2,1)}, u32[]{:S(2)}, u32[]{:S(2)}) %collective-permute-start.13) | collective-permute-done | bytes 1441824 | tf_op jit(solution)/shard_map/ppermute | solution.py:61
  131.2 33.1 %all_gather.3 = bf16[64,2048]{1,0:T(8,128)(2,1)} all-gather(bf16[8,2048]{1,0:T(8,128)(2,1)S(1)} %copy-done.10), channel_id=1, replica_groups=mesh['ep'=8,'fsdp'=4] {'ep'}, dimensions={0}, use_global_device_ids=true | all-gather | bytes 294912 | tf_op jit(solution)/shard_map/all_gather | solution.py:112
  164.3 6.2 %shard_map.96.refs_4_ = bf16[11264,2048]{1,0:T(8,128)(2,1)} custom-call(s32[4]{0:T(128)} %fusion.9.columns_ref, bf16[1408,512]{1,0:T(8,128)(2,1)} %fusion.refs_0_, bf16[1408,512]{1,0:T(8,128)(2,1)} %collective-permute-done.14.refs_1_, bf16[1408,512]{1,0:T(8,128)(2,1)} %collective-permute-done.15.refs_2_, ...), custom_call_target="tpu_custom_call", output_to_operand_aliasing={{}: (5, {})} | custom-call | flops 11534336 | bytes 11534336 | tf_op jit(solution)/shard_map/pallas_call | solution.py:35
  171.8 6.2 %shard_map.97.refs_4_ = bf16[11264,2048]{1,0:T(8,128)(2,1)} custom-call(s32[4]{0:T(128)} %fusion.9.columns_ref, bf16[1408,512]{1,0:T(8,128)(2,1)} %get-tuple-element.66.refs_0_, bf16[1408,512]{1,0:T(8,128)(2,1)} %collective-permute-done.23.refs_1_, bf16[1408,512]{1,0:T(8,128)(2,1)} %collective-permute-done.13.refs_2_, ...), custom_call_target="tpu_custom_call", output_to_operand_aliasing={{}: (5, {})} | custom-call | flops 11534336 | bytes 11534336 | tf_op jit(solution)/shard_map/pallas_call | solution.py:35
  179.2 22.8 %add_multiply_fusion = f32[11264,512]{1,0:T(8,128)} fusion(f32[11264,512]{1,0:T(8,128)} %bitcast.20, f32[11264,512]{1,0:T(8,128)} %bitcast.15), kind=kLoop, calls=%fused_computation | loop fusion | flops 11534336 | bytes 69206016 | tf_op jit(solution)/shard_map/add | solution.py:79
  202.1 3.7 %collective-permute-done.19.refs_2_ = bf16[1408,512]{1,0:T(8,128)(2,1)} collective-permute-done((bf16[1408,512]{1,0:T(8,128)(2,1)}, bf16[1408,512]{1,0:T(8,128)(2,1)}, u32[]{:S(2)}, u32[]{:S(2)}) %collective-permute-start.19) | collective-permute-done | bytes 1441824 | tf_op jit(solution)/shard_map/ppermute | solution.py:61
  205.8 6.4 %shard_map.98.refs_4_ = bf16[11264,2048]{1,0:T(8,128)(2,1)} custom-call(s32[4]{0:T(128)} %fusion.9.columns_ref, bf16[1408,512]{1,0:T(8,128)(2,1)} %get-tuple-element.78.refs_0_, bf16[1408,512]{1,0:T(8,128)(2,1)} %collective-permute-done.20.refs_1_, bf16[1408,512]{1,0:T(8,128)(2,1)} %collective-permute-done.21.refs_2_, ...), custom_call_target="tpu_custom_call", output_to_operand_aliasing={{}: (5, {})} | custom-call | flops 11534336 | bytes 11534336 | tf_op jit(solution)/shard_map/pallas_call | solution.py:35
  213.6 4.2 %divide_convert_fusion.5 = (bf16[704,512]{1,0:T(8,128)(2,1)}, bf16[704,512]{1,0:T(8,128)(2,1)}) fusion(f32[11264,512]{1,0:T(8,128)} %bitcast.16, f32[11264,512]{1,0:T(8,128)} %bitcast.21, f32[704]{0:T(1024)S(1)} %get-tuple-element.111, f32[704]{0:T(1024)S(1)} %get-tuple-element.112), kind=kLoop, calls=%fused_computation.16 | loop fusion | flops 2883584 | bytes 7214592 | tf_op jit(solution)/shard_map/convert_element_type | solution.py:94
  217.8 18.8 %collective-permute-done.27.refs_2_ = bf16[1408,512]{1,0:T(8,128)(2,1)} collective-permute-done((bf16[1408,512]{1,0:T(8,128)(2,1)S(1)}, bf16[1408,512]{1,0:T(8,128)(2,1)}, u32[]{:S(2)}, u32[]{:S(2)}) %collective-permute-start.27) | collective-permute-done | bytes 1441824 | tf_op jit(solution)/shard_map/ppermute | solution.py:61
  236.7 30.0 %collective-permute-done.25.refs_2_ = bf16[1408,512]{1,0:T(8,128)(2,1)} collective-permute-done((bf16[1408,512]{1,0:T(8,128)(2,1)S(1)}, bf16[1408,512]{1,0:T(8,128)(2,1)}, u32[]{:S(2)}, u32[]{:S(2)}) %collective-permute-start.25) | collective-permute-done | bytes 1441824 | tf_op jit(solution)/shard_map/ppermute | solution.py:61
  267.2 6.2 %shard_map.99.refs_4_ = bf16[11264,2048]{1,0:T(8,128)(2,1)} custom-call(s32[4]{0:T(128)} %fusion.9.columns_ref, bf16[1408,512]{1,0:T(8,128)(2,1)} %get-tuple-element.76.refs_0_, bf16[1408,512]{1,0:T(8,128)(2,1)} %collective-permute-done.29.refs_1_, bf16[1408,512]{1,0:T(8,128)(2,1)} %collective-permute-done.19.refs_2_, ...), custom_call_target="tpu_custom_call", output_to_operand_aliasing={{}: (5, {})} | custom-call | flops 11534336 | bytes 11534336 | tf_op jit(solution)/shard_map/pallas_call | solution.py:35
  274.3 6.4 %shard_map.100.refs_4_ = bf16[11264,2048]{1,0:T(8,128)(2,1)} custom-call(s32[4]{0:T(128)} %fusion.9.columns_ref, bf16[1408,512]{1,0:T(8,128)(2,1)} %copy-done.1, bf16[1408,512]{1,0:T(8,128)(2,1)} %collective-permute-done.26.refs_1_, bf16[1408,512]{1,0:T(8,128)(2,1)} %collective-permute-done.27.refs_2_, ...), custom_call_target="tpu_custom_call", output_to_operand_aliasing={{}: (5, {})} | custom-call | flops 11534336 | bytes 11534336 | tf_op jit(solution)/shard_map/pallas_call | solution.py:35
  281.8 10.9 %collective-permute-done.35.refs_2_ = bf16[704,512]{1,0:T(8,128)(2,1)} collective-permute-done((bf16[704,512]{1,0:T(8,128)(2,1)}, bf16[704,512]{1,0:T(8,128)(2,1)}, u32[]{:S(2)}, u32[]{:S(2)}) %collective-permute-start.35) | collective-permute-done | bytes 720928 | tf_op jit(solution)/shard_map/ppermute | solution.py:61
  293.3 14.0 %collective-permute-done.32.refs_2_ = bf16[704,512]{1,0:T(8,128)(2,1)} collective-permute-done((bf16[704,512]{1,0:T(8,128)(2,1)S(1)}, bf16[704,512]{1,0:T(8,128)(2,1)}, u32[]{:S(2)}, u32[]{:S(2)}) %collective-permute-start.32) | collective-permute-done | bytes 720928 | tf_op jit(solution)/shard_map/ppermute | solution.py:61
  307.9 6.2 %shard_map.101.refs_4_ = bf16[11264,2048]{1,0:T(8,128)(2,1)} custom-call(s32[4]{0:T(128)} %fusion.9.columns_ref, bf16[1408,512]{1,0:T(8,128)(2,1)} %copy-done, bf16[1408,512]{1,0:T(8,128)(2,1)} %collective-permute-done.37.refs_1_, bf16[1408,512]{1,0:T(8,128)(2,1)} %collective-permute-done.25.refs_2_, ...), custom_call_target="tpu_custom_call", output_to_operand_aliasing={{}: (5, {})} | custom-call | flops 11534336 | bytes 11534336 | tf_op jit(solution)/shard_map/pallas_call | solution.py:35
  314.2 3.7 %shard_map.102.refs_4_ = bf16[11264,2048]{1,0:T(8,128)(2,1)} custom-call(s32[4]{0:T(128)} %fusion.9.columns_ref, bf16[704,512]{1,0:T(8,128)(2,1)} %get-tuple-element.97.refs_0_, bf16[704,512]{1,0:T(8,128)(2,1)} %collective-permute-done.34.refs_1_, bf16[704,512]{1,0:T(8,128)(2,1)} %collective-permute-done.35.refs_2_, ...), custom_call_target="tpu_custom_call", output_to_operand_aliasing={{}: (5, {})} | custom-call | flops 5767168 | bytes 5767168 | tf_op jit(solution)/shard_map/pallas_call | solution.py:35
  (123 shorter events, 35.3 us)
Async XLA Ops:
  36.0 33.4 %collective-permute-start.10 = (bf16[704,512]{1,0:T(8,128)(2,1)}, bf16[704,512]{1,0:T(8,128)(2,1)}, u32[]{:S(2)}, u32[]{:S(2)}) collective-permute-start(bf16[704,512]{1,0:T(8,128)(2,1)} %get-tuple-element.63.refs_0_), channel_id=1, source_target_pairs={{0,1},{1,0},{2,3},{3,2},{4,5},{5,4},{6,7},{7,6},{8,9},{9,8},{10,11... | collective-permute-start | bytes 2162696 | tf_op jit(solution)/shard_map/ppermute | solution.py:61
  38.5 30.9 %collective-permute-start.9 = (bf16[704,512]{1,0:T(8,128)(2,1)}, bf16[704,512]{1,0:T(8,128)(2,1)}, u32[]{:S(2)}, u32[]{:S(2)}) collective-permute-start(bf16[704,512]{1,0:T(8,128)(2,1)} %get-tuple-element.61.refs_0_), channel_id=1, source_target_pairs={{0,2},{1,3},{2,0},{3,1},{4,6},{5,7},{6,4},{7,5},{8,10},{9,11},{10,... | collective-permute-start | bytes 2162696 | tf_op jit(solution)/shard_map/ppermute | solution.py:61
  53.9 46.3 %collective-permute-start.15 = (bf16[1408,512]{1,0:T(8,128)(2,1)}, bf16[1408,512]{1,0:T(8,128)(2,1)}, u32[]{:S(2)}, u32[]{:S(2)}) collective-permute-start(bf16[1408,512]{1,0:T(8,128)(2,1)} %fusion.refs_0_), channel_id=1, source_target_pairs={{0,2},{1,3},{2,0},{3,1},{4,6},{5,7},{6,4},{7,5},{8,10},{9,11},{10,... | collective-permute-start | bytes 4325384 | tf_op jit(solution)/shard_map/ppermute | solution.py:61
  73.0 58.1 %collective-permute-start.13 = (bf16[1408,512]{1,0:T(8,128)(2,1)}, bf16[1408,512]{1,0:T(8,128)(2,1)}, u32[]{:S(2)}, u32[]{:S(2)}) collective-permute-start(bf16[1408,512]{1,0:T(8,128)(2,1)} %get-tuple-element.66.refs_0_), channel_id=1, source_target_pairs={{0,2},{1,3},{2,0},{3,1},{4,6},{5,7},{6,4},{7,5},{8,10},{9,11},{10,... | collective-permute-start | bytes 4325384 | tf_op jit(solution)/shard_map/ppermute | solution.py:61
  73.9 26.4 %collective-permute-start.17 = (bf16[704,512]{1,0:T(8,128)(2,1)}, bf16[704,512]{1,0:T(8,128)(2,1)}, u32[]{:S(2)}, u32[]{:S(2)}) collective-permute-start(bf16[704,512]{1,0:T(8,128)(2,1)} %get-tuple-element.61.refs_0_), channel_id=1, source_target_pairs={{0,1},{1,0},{2,3},{3,2},{4,5},{5,4},{6,7},{7,6},{8,9},{9,8},{10,11... | collective-permute-start | bytes 2162696 | tf_op jit(solution)/shard_map/ppermute | solution.py:61
  73.9 26.4 %collective-permute-start.18 = (bf16[704,512]{1,0:T(8,128)(2,1)}, bf16[704,512]{1,0:T(8,128)(2,1)}, u32[]{:S(2)}, u32[]{:S(2)}) collective-permute-start(bf16[704,512]{1,0:T(8,128)(2,1)} %collective-permute-done.9.refs_2_), channel_id=1, source_target_pairs={{0,1},{1,0},{2,3},{3,2},{4,5},{5,4},{6,7},{7,6},{8,9},{9,8},{10,11... | collective-permute-start | bytes 2162696 | tf_op jit(solution)/shard_map/ppermute | solution.py:61
  74.4 89.9 %collective-permute-start.14 = (bf16[1408,512]{1,0:T(8,128)(2,1)}, bf16[1408,512]{1,0:T(8,128)(2,1)}, u32[]{:S(2)}, u32[]{:S(2)}) collective-permute-start(bf16[1408,512]{1,0:T(8,128)(2,1)} %fusion.refs_0_), channel_id=1, source_target_pairs={{0,1},{1,0},{2,3},{3,2},{4,5},{5,4},{6,7},{7,6},{8,9},{9,8},{10,11... | collective-permute-start | bytes 4325384 | tf_op jit(solution)/shard_map/ppermute | solution.py:61
  100.2 64.0 %collective-permute-start.16 = (bf16[1408,512]{1,0:T(8,128)(2,1)}, bf16[1408,512]{1,0:T(8,128)(2,1)}, u32[]{:S(2)}, u32[]{:S(2)}) collective-permute-start(bf16[1408,512]{1,0:T(8,128)(2,1)} %collective-permute-done.15.refs_2_), channel_id=1, source_target_pairs={{0,1},{1,0},{2,3},{3,2},{4,5},{5,4},{6,7},{7,6},{8,9},{9,8},{10,11... | collective-permute-start | bytes 4325384 | tf_op jit(solution)/shard_map/ppermute | solution.py:61
  103.9 66.6 %collective-permute-start.21 = (bf16[1408,512]{1,0:T(8,128)(2,1)}, bf16[1408,512]{1,0:T(8,128)(2,1)}, u32[]{:S(2)}, u32[]{:S(2)}) collective-permute-start(bf16[1408,512]{1,0:T(8,128)(2,1)} %get-tuple-element.78.refs_0_), channel_id=1, source_target_pairs={{0,2},{1,3},{2,0},{3,1},{4,6},{5,7},{6,4},{7,5},{8,10},{9,11},{10,... | collective-permute-start | bytes 4325384 | tf_op jit(solution)/shard_map/ppermute | solution.py:61
  104.8 67.0 %collective-permute-start.23 = (bf16[1408,512]{1,0:T(8,128)(2,1)}, bf16[1408,512]{1,0:T(8,128)(2,1)}, u32[]{:S(2)}, u32[]{:S(2)}) collective-permute-start(bf16[1408,512]{1,0:T(8,128)(2,1)} %get-tuple-element.66.refs_0_), channel_id=1, source_target_pairs={{0,1},{1,0},{2,3},{3,2},{4,5},{5,4},{6,7},{7,6},{8,9},{9,8},{10,11... | collective-permute-start | bytes 4325384 | tf_op jit(solution)/shard_map/ppermute | solution.py:61
  131.1 40.7 %collective-permute-start.24 = (bf16[1408,512]{1,0:T(8,128)(2,1)}, bf16[1408,512]{1,0:T(8,128)(2,1)}, u32[]{:S(2)}, u32[]{:S(2)}) collective-permute-start(bf16[1408,512]{1,0:T(8,128)(2,1)} %collective-permute-done.13.refs_2_), channel_id=1, source_target_pairs={{0,1},{1,0},{2,3},{3,2},{4,5},{5,4},{6,7},{7,6},{8,9},{9,8},{10,11... | collective-permute-start | bytes 4325384 | tf_op jit(solution)/shard_map/ppermute | solution.py:61
  164.2 41.5 %collective-permute-start.20 = (bf16[1408,512]{1,0:T(8,128)(2,1)}, bf16[1408,512]{1,0:T(8,128)(2,1)}, u32[]{:S(2)}, u32[]{:S(2)}) collective-permute-start(bf16[1408,512]{1,0:T(8,128)(2,1)} %get-tuple-element.78.refs_0_), channel_id=1, source_target_pairs={{0,1},{1,0},{2,3},{3,2},{4,5},{5,4},{6,7},{7,6},{8,9},{9,8},{10,11... | collective-permute-start | bytes 4325384 | tf_op jit(solution)/shard_map/ppermute | solution.py:61
  170.5 35.3 %collective-permute-start.22 = (bf16[1408,512]{1,0:T(8,128)(2,1)}, bf16[1408,512]{1,0:T(8,128)(2,1)}, u32[]{:S(2)}, u32[]{:S(2)}) collective-permute-start(bf16[1408,512]{1,0:T(8,128)(2,1)} %collective-permute-done.21.refs_2_), channel_id=1, source_target_pairs={{0,1},{1,0},{2,3},{3,2},{4,5},{5,4},{6,7},{7,6},{8,9},{9,8},{10,11... | collective-permute-start | bytes 4325384 | tf_op jit(solution)/shard_map/ppermute | solution.py:61
  171.0 34.8 %collective-permute-start.19 = (bf16[1408,512]{1,0:T(8,128)(2,1)}, bf16[1408,512]{1,0:T(8,128)(2,1)}, u32[]{:S(2)}, u32[]{:S(2)}) collective-permute-start(bf16[1408,512]{1,0:T(8,128)(2,1)} %get-tuple-element.76.refs_0_), channel_id=1, source_target_pairs={{0,2},{1,3},{2,0},{3,1},{4,6},{5,7},{6,4},{7,5},{8,10},{9,11},{10,... | collective-permute-start | bytes 4325384 | tf_op jit(solution)/shard_map/ppermute | solution.py:61
  178.1 58.6 %collective-permute-start.27 = (bf16[1408,512]{1,0:T(8,128)(2,1)S(1)}, bf16[1408,512]{1,0:T(8,128)(2,1)}, u32[]{:S(2)}, u32[]{:S(2)}) collective-permute-start(bf16[1408,512]{1,0:T(8,128)(2,1)S(1)} %get-tuple-element.90.refs_0_), channel_id=1, source_target_pairs={{0,2},{1,3},{2,0},{3,1},{4,6},{5,7},{6,4},{7,5},{8,10},{9,11},{10,... | collective-permute-start | bytes 4325384 | tf_op jit(solution)/shard_map/ppermute | solution.py:61
  212.1 54.5 %collective-permute-start.25 = (bf16[1408,512]{1,0:T(8,128)(2,1)S(1)}, bf16[1408,512]{1,0:T(8,128)(2,1)}, u32[]{:S(2)}, u32[]{:S(2)}) collective-permute-start(bf16[1408,512]{1,0:T(8,128)(2,1)S(1)} %get-tuple-element.88.refs_0_), channel_id=1, source_target_pairs={{0,2},{1,3},{2,0},{3,1},{4,6},{5,7},{6,4},{7,5},{8,10},{9,11},{10,... | collective-permute-start | bytes 4325384 | tf_op jit(solution)/shard_map/ppermute | solution.py:61
  213.0 53.6 %collective-permute-start.29 = (bf16[1408,512]{1,0:T(8,128)(2,1)}, bf16[1408,512]{1,0:T(8,128)(2,1)}, u32[]{:S(2)}, u32[]{:S(2)}) collective-permute-start(bf16[1408,512]{1,0:T(8,128)(2,1)} %get-tuple-element.76.refs_0_), channel_id=1, source_target_pairs={{0,1},{1,0},{2,3},{3,2},{4,5},{5,4},{6,7},{7,6},{8,9},{9,8},{10,11... | collective-permute-start | bytes 4325384 | tf_op jit(solution)/shard_map/ppermute | solution.py:61
  213.1 54.1 %collective-permute-start.30 = (bf16[1408,512]{1,0:T(8,128)(2,1)}, bf16[1408,512]{1,0:T(8,128)(2,1)}, u32[]{:S(2)}, u32[]{:S(2)}) collective-permute-start(bf16[1408,512]{1,0:T(8,128)(2,1)} %collective-permute-done.19.refs_2_), channel_id=1, source_target_pairs={{0,1},{1,0},{2,3},{3,2},{4,5},{5,4},{6,7},{7,6},{8,9},{9,8},{10,11... | collective-permute-start | bytes 4325384 | tf_op jit(solution)/shard_map/ppermute | solution.py:61
  217.8 56.5 %collective-permute-start.26 = (bf16[1408,512]{1,0:T(8,128)(2,1)S(1)}, bf16[1408,512]{1,0:T(8,128)(2,1)}, u32[]{:S(2)}, u32[]{:S(2)}) collective-permute-start(bf16[1408,512]{1,0:T(8,128)(2,1)S(1)} %get-tuple-element.90.refs_0_), channel_id=1, source_target_pairs={{0,1},{1,0},{2,3},{3,2},{4,5},{5,4},{6,7},{7,6},{8,9},{9,8},{10,11... | collective-permute-start | bytes 4325384 | tf_op jit(solution)/shard_map/ppermute | solution.py:61
  236.7 37.6 %collective-permute-start.28 = (bf16[1408,512]{1,0:T(8,128)(2,1)}, bf16[1408,512]{1,0:T(8,128)(2,1)}, u32[]{:S(2)}, u32[]{:S(2)}) collective-permute-start(bf16[1408,512]{1,0:T(8,128)(2,1)} %collective-permute-done.27.refs_2_), channel_id=1, source_target_pairs={{0,1},{1,0},{2,3},{3,2},{4,5},{5,4},{6,7},{7,6},{8,9},{9,8},{10,11... | collective-permute-start | bytes 4325384 | tf_op jit(solution)/shard_map/ppermute | solution.py:61
  266.7 26.1 %collective-permute-start.37 = (bf16[1408,512]{1,0:T(8,128)(2,1)S(1)}, bf16[1408,512]{1,0:T(8,128)(2,1)}, u32[]{:S(2)}, u32[]{:S(2)}) collective-permute-start(bf16[1408,512]{1,0:T(8,128)(2,1)S(1)} %get-tuple-element.88.refs_0_), channel_id=1, source_target_pairs={{0,1},{1,0},{2,3},{3,2},{4,5},{5,4},{6,7},{7,6},{8,9},{9,8},{10,11... | collective-permute-start | bytes 4325384 | tf_op jit(solution)/shard_map/ppermute | solution.py:61
  266.7 41.3 %collective-permute-start.38 = (bf16[1408,512]{1,0:T(8,128)(2,1)}, bf16[1408,512]{1,0:T(8,128)(2,1)}, u32[]{:S(2)}, u32[]{:S(2)}) collective-permute-start(bf16[1408,512]{1,0:T(8,128)(2,1)} %collective-permute-done.25.refs_2_), channel_id=1, source_target_pairs={{0,1},{1,0},{2,3},{3,2},{4,5},{5,4},{6,7},{7,6},{8,9},{9,8},{10,11... | collective-permute-start | bytes 4325384 | tf_op jit(solution)/shard_map/ppermute | solution.py:61
  280.6 26.7 %collective-permute-start.32 = (bf16[704,512]{1,0:T(8,128)(2,1)S(1)}, bf16[704,512]{1,0:T(8,128)(2,1)}, u32[]{:S(2)}, u32[]{:S(2)}) collective-permute-start(bf16[704,512]{1,0:T(8,128)(2,1)S(1)} %copy-done.2), channel_id=1, source_target_pairs={{0,2},{1,3},{2,0},{3,1},{4,6},{5,7},{6,4},{7,5},{8,10},{9,11},{10,... | collective-permute-start | bytes 2162696 | tf_op jit(solution)/shard_map/ppermute | solution.py:61
  281.8 32.3 %collective-permute-start.34 = (bf16[704,512]{1,0:T(8,128)(2,1)S(1)}, bf16[704,512]{1,0:T(8,128)(2,1)}, u32[]{:S(2)}, u32[]{:S(2)}) collective-permute-start(bf16[704,512]{1,0:T(8,128)(2,1)S(1)} %copy-done.3), channel_id=1, source_target_pairs={{0,1},{1,0},{2,3},{3,2},{4,5},{5,4},{6,7},{7,6},{8,9},{9,8},{10,11... | collective-permute-start | bytes 2162696 | tf_op jit(solution)/shard_map/ppermute | solution.py:61
  (34 other events, 689.7 us)
